TPU v7x, 32 devices: a whole 2x2x4 slice. The times are simulated.
32 devices in a mesh: energy: 16 (over z, x, core), space: 2 (over y).
Axes of the slice: x: 2, y: 2, z: 4, core: 2. Of those that a mesh axis runs over, the one named last changes fastest.
Arguments:
- g_lesser: float32 [2, 256, 2, 256, 256], P(None, 'energy', 'space'), may hold values from -6 to 6
- g_greater: float32 [2, 256, 2, 256, 256], P(None, 'energy', 'space'), may hold values from -6 to 6
- v_diag: float32 [2, 256, 256], P('space'), may hold values from -0.375 to 0.375
- v_upper: float32 [2, 256, 256], P('space'), may hold values from -0.375 to 0.375
Outputs:
- screened: float32 [2, 64, 2, 256, 256], P(None, 'energy', 'space')
All inputs are finite; a program needn't handle non-finite values.
Results may differ from a plain program's by a relative error of at most 0.000098.
Values sent between devices are 32-bit elements; how exact they have to be, the bound alone decides.
A program may use at most 128 MiB of HBM per device.

v0:
```python
import math

import jax
import jax.numpy as jnp
from jax import lax
from jax.sharding import PartitionSpec as P

NW = 64


prefactor = 0.0625


def extended(block, sides, width):
    for axis, dim in sides:
        count = lax.axis_size(axis)
        forward = [(i, i + 1) for i in range(count - 1)]
        backward = [(target, source) for source, target in forward]
        low = lax.ppermute(
            lax.slice_in_dim(block, block.shape[dim] - width, None, axis=dim), axis, forward
        )
        high = lax.ppermute(lax.slice_in_dim(block, 0, width, axis=dim), axis, backward)
        block = jnp.concatenate([low, block, high], axis=dim)
    return block


def from_behind(block, axis, distance):
    devices = range(lax.axis_size(axis))
    route = [(i - distance, i) for i in devices if i - distance in devices]
    return lax.ppermute(block, axis, route)


def tables(count):
    length = 2 * count
    freqs = jnp.arange(length, dtype=jnp.int32)[:, None]
    points = jnp.arange(count, dtype=jnp.int32)[None, :]
    phase = 2.0 * math.pi / length * (freqs * points % length).astype(jnp.float32)
    return (jnp.cos(phase), jnp.sin(phase))


def product(left, right):
    return jnp.dot(left, right, precision=lax.Precision.HIGHEST, preferred_element_type=jnp.float32)


def correlate(lesser, greater, keep):
    count = lesser.shape[1]
    rest = tuple(lesser.shape[2:])
    lesser = lesser.reshape(2, count, -1)
    greater = greater.reshape(2, count, -1)
    cosine, sine = tables(count)
    less_re = product(cosine, lesser[0]) + product(sine, lesser[1])
    less_im = product(cosine, lesser[1]) - product(sine, lesser[0])
    great_re = product(cosine, greater[0]) - product(sine, greater[1])
    great_im = product(cosine, greater[1]) + product(sine, greater[0])
    spec_re = less_re * great_re - less_im * great_im
    spec_im = less_re * great_im + less_im * great_re
    factor = prefactor / (2 * count)
    back_cos = cosine.T[:keep]
    back_sin = sine.T[:keep]
    out_re = (product(back_cos, spec_re) - product(back_sin, spec_im)) * factor
    out_im = (product(back_cos, spec_im) + product(back_sin, spec_re)) * factor
    return jnp.stack([out_re, out_im]).reshape((2, keep) + rest)


def sandwich(left, middle, right):
    halfway = jnp.einsum("rab,...rbd->...rad", left, middle, precision=lax.Precision.HIGHEST)
    return jnp.einsum("...rad,rdf->...raf", halfway, right, precision=lax.Precision.HIGHEST)


def local(g_lesser, g_greater, v_diag, v_upper):
    flipped = jnp.swapaxes(g_greater, 3, 4)
    less_entries, great_entries = (
        lax.all_to_all(g_lesser, "energy", split_axis=3, concat_axis=1, tiled=True),
        lax.all_to_all(flipped, "energy", split_axis=3, concat_axis=1, tiled=True),
    )
    polar_entries = correlate(less_entries, great_entries, NW)
    polar = lax.all_to_all(polar_entries, "energy", split_axis=1, concat_axis=3, tiled=True)
    padded = extended(polar, (("space", 2),), 1)
    upper_prev = from_behind(v_upper, "space", 1)
    uppers_before = jnp.concatenate([upper_prev, v_upper[:-1]], axis=0)
    own_term = sandwich(v_diag, polar, v_diag)
    above_term = sandwich(jnp.swapaxes(uppers_before, 1, 2), padded[:, :, :-2], uppers_before)
    below_term = sandwich(v_upper, padded[:, :, 2:], jnp.swapaxes(v_upper, 1, 2))
    return own_term + above_term + below_term


def solution(mesh):
    in_specs = (
        P(None, "energy", "space", None, None),
        P(None, "energy", "space", None, None),
        P("space", None, None),
        P("space", None, None),
    )
    out_specs = P(None, "energy", "space", None, None)
    return jax.shard_map(local, mesh=mesh, in_specs=in_specs, out_specs=out_specs, check_vma=False)
```

profile of v0, /device:TPU:14, one launch (start us, length us, event | category | flops | bytes accessed | tf_op | source)
XLA Modules:
  0.0 619.1 jit_solution(2947893609046970628)
XLA Ops:
  0.0 0.0 copy-start
  0.0 11.5 %copy.74 = f32[2,16,1,256,256]{4,1,2,0,3:T(8,128)} copy(f32[2,16,1,256,256]{4,3,2,1,0:T(8,128)} %param.4) | data formatting | bytes 16777216 | tf_op args[0]
  11.5 6.2 %all-to-all-start = ((f32[2,16,1,256,256]{4,1,2,0,3:T(8,128)}), f32[2,16,1,256,256]{4,1,2,0,3:T(8,128)}, u32[]{:S(2)}, u32[]{:S(2)}) async-start(f32[2,16,1,256,256]{4,1,2,0,3:T(8,128)} %copy.74), calls=%async_computation | async-start | bytes 16777216 | tf_op jit(solution)/shard_map/all_to_all | solution.py:73
  17.8 10.3 %copy.78 = f32[2,16,1,256,256]{3,1,0,2,4:T(8,128)} copy(f32[2,16,1,256,256]{4,3,2,1,0:T(8,128)} %param.5) | data formatting | bytes 16777216 | tf_op args[1]
  28.0 171.8 %all-to-all-done = f32[2,16,1,256,256]{4,1,2,0,3:T(8,128)} async-done(((f32[2,16,1,256,256]{4,1,2,0,3:T(8,128)}), f32[2,16,1,256,256]{4,1,2,0,3:T(8,128)}, u32[]{:S(2)}, u32[]{:S(2)}) %all-to-all-start) | async-done | bytes 8388640 | tf_op jit(solution)/shard_map/all_to_all | solution.py:73
  199.8 5.2 all-to-all-start.1
  205.1 0.2 fusion.16
  205.3 8.2 %copy.75 = f32[2,16,1,256,256]{4,3,1,0,2:T(8,128)S(1)} copy(f32[2,16,1,256,256]{4,1,2,0,3:T(8,128)} %all-to-all-done) | data formatting | bytes 16777216 | tf_op jit(solution)/shard_map/all_to_all | solution.py:73
  213.6 1.6 fusion.82
  215.2 0.5 copy.76
  215.6 3.8 copy.101
  219.4 0.0 copy-start.2
  219.4 0.5 copy.77
  219.9 4.2 copy.102
  224.1 0.0 copy-done.2
  224.1 9.6 %fusion.41 = f32[512,4096]{1,0:T(8,128)S(1)} fusion(f32[256,4096]{1,0:T(8,128)S(1)} %bitcast.125), kind=kOutput, calls=%fused_computation.52 | convolution fusion | flops 6444285952 | bytes 12582912 | tf_op jit(solution)/shard_map/dot_general | solution.py:42
  233.8 12.8 %fusion.37 = f32[512,4096]{1,0:T(8,128)} fusion(f32[256,4096]{1,0:T(8,128)S(1)} %bitcast.121), kind=kOutput, calls=%fused_computation.50 | convolution fusion | flops 6444285952 | bytes 12582912 | tf_op jit(solution)/shard_map/dot_general | solution.py:42
  246.6 12.1 %convolution_add_fusion.1 = f32[512,4096]{1,0:T(8,128)} fusion(f32[512,4096]{1,0:T(8,128)S(1)} %fusion.41, f32[256,4096]{1,0:T(8,128)S(1)} %bitcast.122), kind=kOutput, calls=%fused_computation.5 | convolution fusion | flops 6446383104 | bytes 20971520 | tf_op jit(solution)/shard_map/dot_general | solution.py:42
  258.7 128.3 %all-to-all-done.1 = f32[2,16,1,256,256]{4,1,0,2,3:T(8,128)} async-done(((f32[2,16,1,256,256]{4,1,0,2,3:T(8,128)}), f32[2,16,1,256,256]{4,1,0,2,3:T(8,128)}, u32[]{:S(2)}, u32[]{:S(2)}) %all-to-all-start.1) | async-done | bytes 8388640 | tf_op jit(solution)/shard_map/all_to_all | solution.py:74
  386.9 8.2 %copy.79 = f32[2,16,1,256,256]{4,3,1,0,2:T(8,128)S(1)} copy(f32[2,16,1,256,256]{4,1,0,2,3:T(8,128)} %all-to-all-done.1) | data formatting | bytes 16777216 | tf_op jit(solution)/shard_map/all_to_all | solution.py:74
  395.2 1.6 fusion.81
  396.8 0.5 copy.80
  397.2 3.8 copy.103
  401.0 9.9 %fusion.39 = f32[512,4096]{1,0:T(8,128)S(1)} fusion(f32[256,4096]{1,0:T(8,128)S(1)} %bitcast.119), kind=kOutput, calls=%fused_computation.51 | convolution fusion | flops 6444285952 | bytes 12582912 | tf_op jit(solution)/shard_map/dot_general | solution.py:42
  410.9 0.4 copy.81
  411.4 4.0 copy.104
  415.3 9.5 %fusion.35 = f32[512,4096]{1,0:T(8,128)S(1)} fusion(f32[256,4096]{1,0:T(8,128)S(1)} %bitcast.123), kind=kOutput, calls=%fused_computation.49 | convolution fusion | flops 6444285952 | bytes 12582912 | tf_op jit(solution)/shard_map/dot_general | solution.py:42
  424.8 12.1 %convolution_subtract_fusion.1 = f32[512,4096]{1,0:T(8,128)} fusion(f32[512,4096]{1,0:T(8,128)S(1)} %fusion.39, f32[256,4096]{1,0:T(8,128)S(1)} %bitcast.124), kind=kOutput, calls=%fused_computation.4 | convolution fusion | flops 6446383104 | bytes 20971520 | tf_op jit(solution)/shard_map/dot_general | solution.py:42
  436.9 11.9 %convolution_add_fusion = f32[512,4096]{1,0:T(8,128)} fusion(f32[512,4096]{1,0:T(8,128)S(1)} %fusion.35, f32[256,4096]{1,0:T(8,128)S(1)} %bitcast.120), kind=kOutput, calls=%fused_computation.2 | convolution fusion | flops 6446383104 | bytes 20971520 | tf_op jit(solution)/shard_map/dot_general | solution.py:42
  448.7 24.6 %multiply_subtract_fusion = (f32[512,4096]{1,0:T(8,128)}, f32[512,4096]{1,0:T(8,128)}) fusion(f32[512,4096]{1,0:T(8,128)} %convolution_add_fusion, f32[512,4096]{1,0:T(8,128)} %convolution_add_fusion.1, f32[512,4096]{1,0:T(8,128)} %convolution_subtract_fusion.1, f32[512,4096]{1,0:T(8,128)} %fusion.37, f32[256,4096]{1,0:T(8,128)} %bitcast.126), kind=kOutput, calls=%fused_computation.1 | convolution fusion | flops 6458966016 | bytes 54525952 | tf_op jit(solution)/shard_map/dot_general | solution.py:42
  473.3 0.0 copy-start.1
  473.3 8.6 %fusion.47 = f32[64,4096]{1,0:T(8,128)S(1)} fusion(f32[512,4096]{1,0:T(8,128)} %get-tuple-element.5, f32[256,512]{1,0:T(8,128)S(1)} %fusion.16), kind=kOutput, calls=%fused_computation.55 | convolution fusion | flops 1610612736 | bytes 9568256 | tf_op jit(solution)/shard_map/dot_general | solution.py:42
  481.9 0.0 copy-done.1
  481.9 0.0 slice-start
  481.9 5.6 fusion.48
  487.5 0.0 slice-start.1
  487.5 5.6 fusion
  493.1 0.3 copy.105
  493.4 0.0 slice-done
  493.4 0.0 slice-done.1
  493.4 5.8 fusion.1
  499.2 0.3 copy.106
  499.5 0.2 pad_maximum_fusion
  499.8 51.9 %all_to_all.48 = f32[2,64,1,16,256]{4,3,0,2,1:T(8,128)S(1)} all-to-all(f32[2,64,1,16,256]{4,3,0,2,1:T(8,128)S(1)} %pad_maximum_fusion), channel_id=1, replica_groups=mesh['energy'=16,'space'=2] {'energy'}, dimensions={1} | all-to-all | bytes 4194304 | tf_op jit(solution)/shard_map/all_to_all | solution.py:77
  551.7 0.2 copy.84
  551.9 0.0 copy-start.3
  551.9 0.2 copy.85
  552.1 1.8 copy.89
  553.9 2.5 collective-permute-start.2
  556.4 1.3 collective-permute-start
  557.7 0.0 copy-done.3
  557.7 1.3 collective-permute-start.1
  559.0 0.0 copy-done
  559.0 3.5 fusion.31
  562.6 3.7 fusion.6
  566.3 35.8 %collective-permute-done.2 = f32[2,4,1,256,256]{3,4,1,0,2:T(8,128)S(1)} collective-permute-done((f32[2,4,1,256,256]{3,4,1,0,2:T(8,128)}, f32[2,4,1,256,256]{3,4,1,0,2:T(8,128)S(1)}, u32[]{:S(2)}, u32[]{:S(2)}) %collective-permute-start.2) | collective-permute-done | bytes 2097184 | tf_op jit(solution)/shard_map/ppermute | solution.py:22
  602.0 1.9 fusion.8
  603.9 3.9 fusion.2
  607.9 3.9 collective-permute-done.1
  611.8 0.0 collective-permute-done
  611.8 1.9 fusion.10
  613.7 5.0 add_bitcast_fusion
  (1 shorter events, 0.0 us)
Async XLA Ops:
  0.0 559.0 %copy-start = (f32[1,256,256]{2,1,0:T(8,128)S(1)}, f32[1,256,256]{2,1,0:T(8,128)}, u32[]{:S(2)}) copy-start(f32[1,256,256]{2,1,0:T(8,128)} %param.6) | copy-start | bytes 786436
  11.5 188.3 %all-to-all-start = ((f32[2,16,1,256,256]{4,1,2,0,3:T(8,128)}), f32[2,16,1,256,256]{4,1,2,0,3:T(8,128)}, u32[]{:S(2)}, u32[]{:S(2)}) async-start(f32[2,16,1,256,256]{4,1,2,0,3:T(8,128)} %copy.74), calls=%async_computation | async-start | bytes 16777216 | tf_op jit(solution)/shard_map/all_to_all | solution.py:73
  199.8 187.1 %all-to-all-start.1 = ((f32[2,16,1,256,256]{4,1,0,2,3:T(8,128)}), f32[2,16,1,256,256]{4,1,0,2,3:T(8,128)}, u32[]{:S(2)}, u32[]{:S(2)}) async-start(f32[2,16,1,256,256]{4,1,0,2,3:T(8,128)} %bitcast.127), calls=%async_computation.1 | async-start | bytes 16777216 | tf_op jit(solution)/shard_map/all_to_all | solution.py:74
  219.4 4.7 copy-start.2
  473.3 8.6 %copy-start.1 = (f32[512,4096]{1,0:T(8,128)S(1)}, f32[512,4096]{1,0:T(8,128)}, u32[]{:S(2)}) copy-start(f32[512,4096]{1,0:T(8,128)} %get-tuple-element.6) | copy-start | bytes 25165828
  481.9 11.5 %slice-start = ((s8[8388608]{0:T(1024)(128)(4,1)}), s8[4194304]{0:T(1024)(128)(4,1)S(1)}, s32[]{:S(2)}) async-start(s8[8388608]{0:T(1024)(128)(4,1)} %bitcast.117), calls=%async_computation.3 | async-start | bytes 8388608
  487.5 5.9 slice-start.1
  551.9 5.8 copy-start.3
  553.9 48.1 %collective-permute-start.2 = (f32[2,4,1,256,256]{3,4,1,0,2:T(8,128)}, f32[2,4,1,256,256]{3,4,1,0,2:T(8,128)S(1)}, u32[]{:S(2)}, u32[]{:S(2)}) collective-permute-start(f32[2,4,1,256,256]{3,4,1,0,2:T(8,128)} %copy.89), channel_id=1, source_target_pairs={{1,0},{3,2},{5,4},{7,6},{9,8},{11,10},{13,12},{15,14},{17,16},{19,... | collective-permute-start | bytes 6291464 | tf_op jit(solution)/shard_map/ppermute | solution.py:22
  556.4 55.4 %collective-permute-start = (f32[2,4,1,256,256]{3,4,1,0,2:T(8,128)}, f32[2,4,1,256,256]{3,4,1,0,2:T(8,128)S(1)}, u32[]{:S(2)}, u32[]{:S(2)}) collective-permute-start(f32[2,4,1,256,256]{3,4,1,0,2:T(8,128)} %copy.89), channel_id=1, source_target_pairs={{0,1},{2,3},{4,5},{6,7},{8,9},{10,11},{12,13},{14,15},{16,17},{18,... | collective-permute-start | bytes 6291464 | tf_op jit(solution)/shard_map/ppermute | solution.py:19
  557.7 54.1 %collective-permute-start.1 = (f32[1,256,256]{2,1,0:T(8,128)S(1)}, f32[1,256,256]{2,1,0:T(8,128)S(1)}, u32[]{:S(2)}, u32[]{:S(2)}) collective-permute-start(f32[1,256,256]{2,1,0:T(8,128)S(1)} %copy-done.3), channel_id=1, source_target_pairs={{0,1},{2,3},{4,5},{6,7},{8,9},{10,11},{12,13},{14,15},{16,17},{18,... | collective-permute-start | bytes 786440 | tf_op jit(solution)/shard_map/ppermute | solution.py:30
where the time goes:
time: 625 us; the launch traced here: 619 us
  waiting for transfers between devices  340 us (54%)
  matrix products  148 us (24%)
  local copies, waits for them, and re-layouts  61.9 us (10%)
  blocking collectives  51.9 us (8%)
  starting transfers between devices  16.6 us (3%)
    all_to_all x1, waiting for transfers between devices, local(): lax.all_to_all(g_lesser, 'energy', split_axis=3, concat_axis=1, tiled=True)  172 us
    all_to_all x1, waiting for transfers between devices, local(): lax.all_to_all(flipped, 'energy', split_axis=3, concat_axis=1, tiled=True)  128 us
    dot_general x12, matrix products, product(): jnp.dot(left, right, precision=lax.Precision.HIGHEST, preferred_element_t...  128 us
    all_to_all x1, blocking collectives, local(): lax.all_to_all(polar_entries, 'energy', split_axis=1, concat_axis=3, tile...  51.9 us
    unnamed x20, local copies, waits for them, and re-layouts  38.2 us
    ppermute x1, waiting for transfers between devices, extended(): lax.ppermute(lax.slice_in_dim(block, 0, width, axis=dim), axis, backward)  35.8 us
    dot_general x3, matrix products, sandwich(): jnp.einsum('...rad,rdf->...raf', halfway, right, precision=lax.Precision....  12.6 us
  transfers between devices with their start and end apart: 5, of which 4 were waited for; matrix products, arithmetic and copies ran while one was open for 12% of the time, Pallas kernels for 0%

commit v1 on v0

v1 whole, which is shorter than its diff:
```python
import functools
import math

import jax
import jax.numpy as jnp
import numpy as np
from jax import lax
from jax.experimental import pallas as pl
from jax.experimental.pallas import tpu as pltpu
from jax.sharding import PartitionSpec as P

NW = 64
PREFACTOR = 0.0625
ROWS = 8
LANES = 128
HIGH = lax.Precision.HIGH


def split_np(table):
    table = np.asarray(table, np.float64)
    high = table.astype(jnp.bfloat16)
    low = (table - high.astype(np.float64)).astype(jnp.bfloat16)
    return np.concatenate([high, low, high], axis=1)


def tables(count, keep):
    length = -(-(count + keep) // 64) * 64
    freqs = np.arange(length)[:, None]
    points = np.arange(count)[None, :]
    phase = 2.0 * math.pi / length * (freqs * points % length)
    cos, sin = np.cos(phase), np.sin(phase)
    factor = PREFACTOR / length
    back_cos, back_sin = cos.T[:keep] * factor, sin.T[:keep] * factor
    lesser = np.block([[cos, sin], [-sin, cos]])
    greater = np.block([[cos, -sin], [sin, cos]])
    back = np.block([[back_cos, -back_sin], [back_sin, back_cos]])
    return [jnp.asarray(split_np(t)) for t in (lesser, greater, back)]


def stacked(value):
    high = value.astype(jnp.bfloat16)
    low = (value - high.astype(jnp.float32)).astype(jnp.bfloat16)
    return jnp.concatenate([high, high, low], axis=0)


def dot(table, value):
    return jnp.dot(table, stacked(value), preferred_element_type=jnp.float32)


def correlate_kernel(
    n, lanes_parts, less_tab, great_tab, back_tab, less, great, out,
    less_buf, great_buf, polar_buf, in_send, in_recv, own_sem, out_send, out_recv, out_own,
):
    me = lax.axis_index("energy")
    sources, buffers = (less, great), (less_buf, great_buf)
    held = less.shape[1]
    kept = out.shape[1]
    chunks = less_buf.shape[0]
    count = less_buf.shape[2]
    keep = polar_buf.shape[2]

    def place(c):
        if isinstance(c, int):
            return c // lanes_parts, pl.ds(c % lanes_parts * LANES, LANES)
        return c // lanes_parts, pl.ds(pl.multiple_of(c % lanes_parts * LANES, LANES), LANES)

    def in_copy(k, c, d):
        peer = lax.rem(me + d, n)
        row, lane = place(c)
        return pltpu.make_async_remote_copy(
            src_ref=sources[k].at[:, :, peer, row, :, lane],
            dst_ref=buffers[k].at[c, :, pl.ds(me * held, held)],
            send_sem=in_send.at[k, c, d],
            recv_sem=in_recv.at[k, c, d],
            device_id={"energy": peer},
            device_id_type=pl.DeviceIdType.MESH,
        )

    def in_own(k, c):
        row, lane = place(c)
        return pltpu.make_async_copy(
            sources[k].at[:, :, me, row, :, lane],
            buffers[k].at[c, :, pl.ds(me * held, held)],
            own_sem.at[k, c],
        )

    def out_copy(c, d):
        peer = lax.rem(me + d, n)
        row, lane = place(c)
        return pltpu.make_async_remote_copy(
            src_ref=polar_buf.at[c, :, pl.ds(peer * kept, kept)],
            dst_ref=out.at[:, :, me, row, :, lane],
            send_sem=out_send.at[c, d],
            recv_sem=out_recv.at[c, d],
            device_id={"energy": peer},
            device_id_type=pl.DeviceIdType.MESH,
        )

    def out_mine(c):
        row, lane = place(c)
        return pltpu.make_async_copy(
            polar_buf.at[c, :, pl.ds(me * kept, kept)], out.at[:, :, me, row, :, lane], out_own.at[c]
        )

    def each(body):
        def step(d, carry):
            body(d)
            return carry
        lax.fori_loop(1, n, step, 0)

    barrier = pltpu.get_barrier_semaphore()
    each(lambda d: pl.semaphore_signal(
        barrier, inc=1, device_id={"energy": lax.rem(me + d, n)}, device_id_type=pl.DeviceIdType.MESH))
    pl.semaphore_wait(barrier, n - 1)

    def send_chunk(c, carry):
        for k in range(2):
            in_own(k, c).start()
            each(lambda d: in_copy(k, c, d).start())
        return carry

    lax.fori_loop(0, chunks, send_chunk, 0)

    def pair(buf, c, i):
        parts = [buf[c, :, :, i + s, :].reshape(2 * count, LANES) for s in range(2)]
        return jnp.concatenate(parts, axis=1)

    def compute_chunk(c, carry):
        for k in range(2):
            in_own(k, c).wait()
            each(lambda d: in_copy(k, c, d).wait_recv())
        for i in range(0, ROWS, 2):
            spec_l = dot(less_tab[...], pair(less_buf, c, i))
            spec_g = dot(great_tab[...], pair(great_buf, c, i))
            half = spec_l.shape[0] // 2
            lr, li, gr, gi = spec_l[:half], spec_l[half:], spec_g[:half], spec_g[half:]
            spec = jnp.concatenate([lr * gr - li * gi, lr * gi + li * gr], axis=0)
            polar = dot(back_tab[...], spec)
            for s in range(2):
                polar_buf[c, :, :, i + s, :] = polar[:, s * LANES:(s + 1) * LANES].reshape(2, keep, LANES)
        out_mine(c).start()
        each(lambda d: out_copy(c, d).start())
        return carry

    lax.fori_loop(0, chunks, compute_chunk, 0)

    def finish(c, carry):
        out_mine(c).wait()
        for k in range(2):
            each(lambda d: in_copy(k, c, d).wait_send())
        each(lambda d: out_copy(c, d).wait())
        return carry

    lax.fori_loop(0, chunks, finish, 0)


def polarization(g_lesser, g_flipped, keep):
    n = lax.axis_size("energy")
    _, held, _, size, width = g_lesser.shape
    count = held * n
    row_parts, lane_parts = size // n // ROWS, width // LANES
    chunks = row_parts * lane_parts
    less = g_lesser.reshape(2, held, n, row_parts, ROWS, width)
    great = g_flipped.reshape(2, held, n, row_parts, ROWS, width)
    tabs = tables(count, keep)
    any_spec = pl.BlockSpec(memory_space=pl.ANY)
    dma = pltpu.SemaphoreType.DMA
    out = pl.pallas_call(
        functools.partial(correlate_kernel, n, lane_parts),
        out_shape=jax.ShapeDtypeStruct((2, keep // n, n, row_parts, ROWS, width), jnp.float32),
        in_specs=[pl.BlockSpec(memory_space=pltpu.VMEM)] * 3 + [any_spec] * 2,
        out_specs=any_spec,
        scratch_shapes=[
            pltpu.VMEM((chunks, 2, count, ROWS, LANES), jnp.float32),
            pltpu.VMEM((chunks, 2, count, ROWS, LANES), jnp.float32),
            pltpu.VMEM((chunks, 2, keep, ROWS, LANES), jnp.float32),
            dma((2, chunks, n)), dma((2, chunks, n)), dma((2, chunks)),
            dma((chunks, n)), dma((chunks, n)), dma((chunks,)),
        ],
        compiler_params=pltpu.CompilerParams(
            collective_id=0, has_side_effects=True, vmem_limit_bytes=56 * 2**20),
    )(*tabs, less, great)
    return out.reshape(2, keep // n, 1, size, width)


def shifted(block, axis, distance):
    devices = range(lax.axis_size(axis))
    return lax.ppermute(block, axis, [(i - distance, i) for i in devices if i - distance in devices])


def sandwich(left, middle, right):
    halfway = jnp.einsum("ab,cwbd->cwad", left, middle, precision=HIGH)
    return jnp.einsum("cwad,df->cwaf", halfway, right, precision=HIGH)


def local(g_lesser, g_greater, v_diag, v_upper):
    polar = polarization(g_lesser, jnp.swapaxes(g_greater, 3, 4), NW)[:, :, 0]
    rows = lax.axis_size("space")
    before = shifted(v_upper, "space", 1)[0]
    diag, upper = v_diag[0], v_upper[0]
    if rows == 2:
        other = lax.ppermute(polar, "space", [(0, 1), (1, 0)])
        coupling = jnp.where(lax.axis_index("space") == 0, upper, before.T)
        total = sandwich(diag, polar, diag) + sandwich(coupling, other, coupling.T)
    else:
        above, below = shifted(polar, "space", 1), shifted(polar, "space", -1)
        total = sandwich(diag, polar, diag)
        total = total + sandwich(before.T, above, before) + sandwich(upper, below, upper.T)
    return total[:, :, None]


def solution(mesh):
    in_specs = (
        P(None, "energy", "space", None, None),
        P(None, "energy", "space", None, None),
        P("space", None, None),
        P("space", None, None),
    )
    out_specs = P(None, "energy", "space", None, None)
    return jax.shard_map(local, mesh=mesh, in_specs=in_specs, out_specs=out_specs, check_vma=False)
```

time: 625 us -> 483 us (0.77)
  Pallas kernels: 0 us -> 416 us
  waiting for transfers between devices: 340 us -> 48.2 us
  matrix products: 148 us -> 7.09 us
  local copies, waits for them, and re-layouts: 61.9 us -> 8.87 us
  blocking collectives: 51.9 us -> 0 us
  starting transfers between devices: 16.6 us -> 1.85 us
    pallas_call x0 -> x1, Pallas kernels: none -> 416 us  [polarization(): pl.pallas_call(functools.partial(correlate_kernel, n, lane_parts), out_sh...]
    all_to_all x2 -> x0, waiting for transfers between devices: 300 us -> none  [the longest x1 172 us: local(): lax.all_to_all(g_lesser, 'energy', split_axis=3, concat_axis=1, tiled=True)]
    dot_general x18 -> x4, matrix products: 148 us -> 7.09 us  [the longest x2 3.69 us: sandwich(): halfway = jnp.einsum('ab,cwbd->cwad', left, middle, precision=HIGH)]
    all_to_all x1 -> x0, blocking collectives: 51.9 us -> none  [local(): lax.all_to_all(polar_entries, 'energy', split_axis=1, concat_axis=3, tile...]
    unnamed x20 -> x5, local copies, waits for them, and re-layouts: 38.2 us -> 0.14 us
    all_to_all x5 -> x0, local copies, waits for them, and re-layouts: 18.7 us -> none  [the longest x1 8.24 us: local(): lax.all_to_all(g_lesser, 'energy', split_axis=3, concat_axis=1, tiled=True)]
    all_to_all x2 -> x0, starting transfers between devices: 11.5 us -> none  [the longest x1 6.24 us: local(): lax.all_to_all(g_lesser, 'energy', split_axis=3, concat_axis=1, tiled=True)]
    transpose x0 -> x1, local copies, waits for them, and re-layouts: none -> 8.74 us  [local(): polar = polarization(g_lesser, jnp.swapaxes(g_greater, 3, 4), NW)[:, :, 0]]
  transfers between devices with their start and end apart: 5 -> 2, of which waited for: 4 -> 1; matrix products, arithmetic and copies ran while one was open for 12% -> 1% of each run, Pallas kernels for 0% -> 0%
where the time goes in v1:
time: 483 us
  Pallas kernels  416 us (86%)
  waiting for transfers between devices  48.2 us (10%)
  local copies, waits for them, and re-layouts  8.87 us (2%)
  matrix products  7.09 us (1%)
    pallas_call x1, Pallas kernels, polarization(): pl.pallas_call(functools.partial(correlate_kernel, n, lane_parts), out_sh...  416 us
    ppermute x1, waiting for transfers between devices, shifted(): lax.ppermute(block, axis, [(i - distance, i) for i in devices if i - dist...  48.2 us
  transfers between devices with their start and end apart: 2, of which 1 were waited for; matrix products, arithmetic and copies ran while one was open for 1% of the time, Pallas kernels for 0%

profile of v1, /device:TPU:14, one launch (start us, length us, event | category | flops | bytes accessed | tf_op | source)
XLA Modules:
  0.0 482.5 jit_solution(17038065048193342624)
XLA Ops:
  0.0 0.0 copy-start
  0.0 8.7 %copy.11 = f32[2,16,1,256,256]{4,3,1,0,2:T(8,128)} copy(f32[2,16,1,256,256]{3,4,2,1,0:T(8,128)} %bitcast.55) | data formatting | bytes 16777216 | tf_op jit(solution)/shard_map/transpose | solution.py:197
  8.7 0.0 copy-start.1
  8.7 416.4 %shard_map.73 = f32[2,4,16,2,8,256]{5,4,3,2,1,0:T(8,128)} custom-call(bf16[640,1536]{1,0:T(8,128)(2,1)} %constant.12.clone.less_tab, bf16[640,1536]{1,0:T(8,128)(2,1)} %constant.13.clone.great_tab, bf16[128,1920]{1,0:T(8,128)(2,1)} %constant.14.clone.back_tab, f32[2,16,16,2,8,256]{5,4,3,2,1,0:T(8,128)} %bitcast.56, f32[2,16,16,2,8,256]{5,4,3,2,1,0:T(8,128)} %bitcast.52), custom_call_target="tpu_custom_call" | custom-call | tf_op jit(solution)/shard_map/pallas_call | solution.py:168
  425.2 0.6 collective-permute-start
  425.7 0.0 copy-done.1
  425.7 0.1 copy.12
  425.9 1.3 collective-permute-start.1
  427.2 0.0 copy-done
  427.2 2.6 fusion.10
  429.8 1.0 fusion.2
  430.8 48.2 %collective-permute-done.1 = f32[1,256,256]{1,2,0:T(8,128)S(1)} collective-permute-done((f32[1,256,256]{1,2,0:T(8,128)S(1)}, f32[1,256,256]{1,2,0:T(8,128)S(1)}, u32[]{:S(2)}, u32[]{:S(2)}) %collective-permute-start.1) | collective-permute-done | bytes 262176 | tf_op jit(solution)/shard_map/ppermute | solution.py:188
  479.1 0.0 collective-permute-done
  479.1 1.1 fusion.7
  480.1 2.4 add_bitcast_fusion
Async XLA Ops:
  0.0 427.2 %copy-start = (f32[1,256,256]{2,1,0:T(8,128)S(1)}, f32[1,256,256]{2,1,0:T(8,128)}, u32[]{:S(2)}) copy-start(f32[1,256,256]{2,1,0:T(8,128)} %param.9) | copy-start | bytes 786436
  8.7 417.0 %copy-start.1 = (f32[1,256,256]{2,1,0:T(8,128)S(1)}, f32[1,256,256]{2,1,0:T(8,128)}, u32[]{:S(2)}) copy-start(f32[1,256,256]{2,1,0:T(8,128)} %param.10) | copy-start | bytes 786436
  425.2 53.9 %collective-permute-start = (f32[2,4,256,256]{3,2,1,0:T(8,128)}, f32[2,4,256,256]{3,2,1,0:T(8,128)S(1)}, u32[]{:S(2)}, u32[]{:S(2)}) collective-permute-start(f32[2,4,256,256]{3,2,1,0:T(8,128)} %bitcast.53), channel_id=1, source_target_pairs={{0,1},{1,0},{2,3},{3,2},{4,5},{5,4},{6,7},{7,6},{8,9},{9,8},{10,11... | collective-permute-start | bytes 6291464 | tf_op jit(solution)/shard_map/ppermute | solution.py:202
  425.9 53.2 %collective-permute-start.1 = (f32[1,256,256]{1,2,0:T(8,128)S(1)}, f32[1,256,256]{1,2,0:T(8,128)S(1)}, u32[]{:S(2)}, u32[]{:S(2)}) collective-permute-start(f32[1,256,256]{1,2,0:T(8,128)S(1)} %copy.12), channel_id=1, source_target_pairs={{0,1},{2,3},{4,5},{6,7},{8,9},{10,11},{12,13},{14,15},{16,17},{18,... | collective-permute-start | bytes 786440 | tf_op jit(solution)/shard_map/ppermute | solution.py:188

commit v2 on v1

v2 whole, which is shorter than its diff:
```python
import functools
import math

import jax
import jax.numpy as jnp
import numpy as np
from jax import lax
from jax.experimental import pallas as pl
from jax.experimental.pallas import tpu as pltpu
from jax.sharding import PartitionSpec as P

NW = 64
PREFACTOR = 0.0625
ROWS = 8
HIGH = lax.Precision.HIGH


def split_np(table):
    table = np.asarray(table, np.float64)
    high = table.astype(jnp.bfloat16)
    low = (table - high.astype(np.float64)).astype(jnp.bfloat16)
    return np.concatenate([high, low, high], axis=1)


def tables(keep):
    length = 2 * keep

    def forward(start, sign):
        phase = 2.0 * math.pi / length * (np.outer(np.arange(length), np.arange(start, start + keep)) % length)
        cos, sin = np.cos(phase), sign * np.sin(phase)
        return np.block([[cos, sin], [-sin, cos]])

    phase = 2.0 * math.pi / length * (np.outer(np.arange(keep), np.arange(length)) % length)
    cos, sin = np.cos(phase) * (PREFACTOR / length), np.sin(phase) * (PREFACTOR / length)
    back = np.block([[cos, -sin], [sin, cos]])
    wide = [np.concatenate([forward(0, sign), forward(keep, sign)], axis=1) for sign in (1, -1)]
    narrow = [forward(0, sign) for sign in (1, -1)]
    return [jnp.asarray(split_np(t)) for t in (*wide, *narrow, back)]


def stacked(value):
    high = value.astype(jnp.bfloat16)
    low = (value - high.astype(jnp.float32)).astype(jnp.bfloat16)
    return jnp.concatenate([high, high, low], axis=0)


def dot(table, value):
    return jnp.dot(table, stacked(value), preferred_element_type=jnp.float32)


def correlate_kernel(
    n, group, less_wide, great_wide, less_narrow, great_narrow, back_tab, less, great, out,
    less_buf, great_buf, halo_buf, polar_buf,
    in_send, in_recv, own_sem, halo_send, halo_recv, out_send, out_recv, out_own,
):
    me = lax.axis_index("energy")
    mine, share = me // group, lax.rem(me, group)
    groups = n // group
    sources, buffers = (less, great), (less_buf, great_buf)
    held = less.shape[1]
    kept = out.shape[2]
    stages = less_buf.shape[0]
    keep = polar_buf.shape[2]
    half = less_buf.shape[4] // 2
    mesh_id = pl.DeviceIdType.MESH

    def in_copy(k, q, d):
        other = lax.rem(share + d, group)
        return pltpu.make_async_remote_copy(
            src_ref=sources[k].at[:, :, other, q],
            dst_ref=buffers[k].at[q, :, pl.ds(share * held, held)],
            send_sem=in_send.at[k, q, d],
            recv_sem=in_recv.at[k, q, d],
            device_id={"energy": mine * group + other},
            device_id_type=mesh_id,
        )

    def in_own(k, q):
        return pltpu.make_async_copy(
            sources[k].at[:, :, share, q], buffers[k].at[q, :, pl.ds(share * held, held)], own_sem.at[k, q]
        )

    def halo_copy(k, q):
        lanes = pl.ds((1 - k) * half, half)
        peer = lax.rem(me + (group if k else n - group), n)
        return pltpu.make_async_remote_copy(
            src_ref=buffers[k].at[q, :, :, :, lanes],
            dst_ref=halo_buf.at[q, :, :, :, lanes],
            send_sem=halo_send.at[k, q],
            recv_sem=halo_recv.at[k, q],
            device_id={"energy": peer},
            device_id_type=mesh_id,
        )

    sends = (mine > 0, mine < groups - 1)
    receives = (mine < groups - 1, mine > 0)

    def out_copy(q, d):
        peer = lax.rem(me + d, n)
        return pltpu.make_async_remote_copy(
            src_ref=polar_buf.at[q, :, pl.ds(peer * kept, kept)],
            dst_ref=out.at[mine, :, :, share, q],
            send_sem=out_send.at[q, d],
            recv_sem=out_recv.at[q, d],
            device_id={"energy": peer},
            device_id_type=mesh_id,
        )

    def out_mine(q):
        return pltpu.make_async_copy(
            polar_buf.at[q, :, pl.ds(me * kept, kept)], out.at[mine, :, :, share, q], out_own.at[q]
        )

    def each(first, last, body):
        def step(d, carry):
            body(d)
            return carry
        lax.fori_loop(first, last, step, 0)

    barrier = pltpu.get_barrier_semaphore()
    each(1, n, lambda d: pl.semaphore_signal(
        barrier, inc=1, device_id={"energy": lax.rem(me + d, n)}, device_id_type=mesh_id))
    pl.semaphore_wait(barrier, n - 1)

    def send_stage(q):
        for k in range(2):
            in_own(k, q).start()
            each(1, group, lambda d: in_copy(k, q, d).start())

    each(0, stages, send_stage)

    def forward_stage(q):
        for k in range(2):
            in_own(k, q).wait()
            each(1, group, lambda d: in_copy(k, q, d).wait_recv())

            @pl.when(sends[k])
            def _():
                halo_copy(k, q).start()

    def pair(buf, q, i, j):
        lanes = slice(j * half, (j + 1) * half)
        return jnp.concatenate([buf[q, :, :, i + s, lanes].reshape(2 * keep, half) for s in range(2)], axis=1)

    def compute_stage(q):
        for k in range(2):
            @pl.when(receives[k])
            def _():
                halo_copy(k, q).wait_recv()

            @pl.when(jnp.logical_not(receives[k]))
            def _():
                lanes = slice((1 - k) * half, (2 - k) * half)
                halo_buf[q, :, :, :, lanes] = jnp.zeros((2, keep, ROWS, half), jnp.float32)

        for i in range(0, ROWS, 2):
            for j in range(2):
                less_x, great_x = pair(less_buf, q, i, j), pair(great_buf, q, i, j)
                halo_x = pair(halo_buf, q, i, j)
                if j == 0:
                    spec_l = dot(less_narrow[...], less_x)
                    spec_g = dot(great_wide[...], jnp.concatenate([great_x, halo_x], axis=0))
                else:
                    spec_l = dot(less_wide[...], jnp.concatenate([less_x, halo_x], axis=0))
                    spec_g = dot(great_narrow[...], great_x)
                mid = spec_l.shape[0] // 2
                lr, li, gr, gi = spec_l[:mid], spec_l[mid:], spec_g[:mid], spec_g[mid:]
                spec = jnp.concatenate([lr * gr - li * gi, lr * gi + li * gr], axis=0)
                polar = dot(back_tab[...], spec)
                for s in range(2):
                    polar_buf[q, :, :, i + s, j * half:(j + 1) * half] = (
                        polar[:, s * half:(s + 1) * half].reshape(2, keep, half))
        out_mine(q).start()
        each(1, n, lambda d: out_copy(q, d).start())

    forward_stage(0)

    def step(q):
        @pl.when(q < stages - 1)
        def _():
            forward_stage(q + 1)
        compute_stage(q)

    each(0, stages, step)

    def finish(q):
        out_mine(q).wait()
        for k in range(2):
            each(1, group, lambda d: in_copy(k, q, d).wait_send())

            @pl.when(sends[k])
            def _():
                halo_copy(k, q).wait_send()
        each(1, n, lambda d: out_copy(q, d).wait())

    each(0, stages, finish)


def polarization(g_lesser, g_flipped, keep):
    n = lax.axis_size("energy")
    _, held, _, size, width = g_lesser.shape
    group = keep // held
    stages = size // group // ROWS
    less = g_lesser.reshape(2, held, group, stages, ROWS, width)
    great = g_flipped.reshape(2, held, group, stages, ROWS, width)
    tabs = tables(keep)
    any_spec = pl.BlockSpec(memory_space=pl.ANY)
    dma = pltpu.SemaphoreType.DMA
    block = pltpu.VMEM((stages, 2, keep, ROWS, width), jnp.float32)
    out = pl.pallas_call(
        functools.partial(correlate_kernel, n, group),
        out_shape=jax.ShapeDtypeStruct((n // group, 2, keep // n, group, stages, ROWS, width), jnp.float32),
        in_specs=[pl.BlockSpec(memory_space=pltpu.VMEM)] * len(tabs) + [any_spec] * 2,
        out_specs=any_spec,
        scratch_shapes=[
            block, block, block, block,
            dma((2, stages, group)), dma((2, stages, group)), dma((2, stages)),
            dma((2, stages)), dma((2, stages)),
            dma((stages, n)), dma((stages, n)), dma((stages,)),
        ],
        compiler_params=pltpu.CompilerParams(
            collective_id=0, has_side_effects=True, vmem_limit_bytes=56 * 2**20),
    )(*tabs, less, great)
    return jnp.sum(out, axis=0).reshape(2, keep // n, 1, size, width)


def shifted(block, axis, distance):
    devices = range(lax.axis_size(axis))
    return lax.ppermute(block, axis, [(i - distance, i) for i in devices if i - distance in devices])


def sandwich(left, middle, right):
    halfway = jnp.einsum("ab,cwbd->cwad", left, middle, precision=HIGH)
    return jnp.einsum("cwad,df->cwaf", halfway, right, precision=HIGH)


def local(g_lesser, g_greater, v_diag, v_upper):
    polar = polarization(g_lesser, jnp.swapaxes(g_greater, 3, 4), NW)[:, :, 0]
    rows = lax.axis_size("space")
    before = shifted(v_upper, "space", 1)[0]
    diag, upper = v_diag[0], v_upper[0]
    if rows == 2:
        other = lax.ppermute(polar, "space", [(0, 1), (1, 0)])
        coupling = jnp.where(lax.axis_index("space") == 0, upper, before.T)
        total = sandwich(diag, polar, diag) + sandwich(coupling, other, coupling.T)
    else:
        above, below = shifted(polar, "space", 1), shifted(polar, "space", -1)
        total = sandwich(diag, polar, diag)
        total = total + sandwich(before.T, above, before) + sandwich(upper, below, upper.T)
    return total[:, :, None]


def solution(mesh):
    in_specs = (
        P(None, "energy", "space", None, None),
        P(None, "energy", "space", None, None),
        P("space", None, None),
        P("space", None, None),
    )
    out_specs = P(None, "energy", "space", None, None)
    return jax.shard_map(local, mesh=mesh, in_specs=in_specs, out_specs=out_specs, check_vma=False)
```

time: 483 us -> 382 us (0.79)
  Pallas kernels: 416 us -> 307 us
    pallas_call x1, Pallas kernels: 416 us -> 307 us  [polarization(): pl.pallas_call(functools.partial(correlate_kernel, n, group), out_shape=j...]
where the time goes in v2:
time: 382 us; the launch traced here: 377 us
  Pallas kernels  307 us (80%)
  waiting for transfers between devices  48.1 us (13%)
  local copies, waits for them, and re-layouts  8.86 us (2%)
  matrix products  7.08 us (2%)
  other arithmetic  4.4 us (1%)
    pallas_call x1, Pallas kernels, polarization(): pl.pallas_call(functools.partial(correlate_kernel, n, group), out_shape=j...  307 us
    ppermute x1, waiting for transfers between devices, shifted(): lax.ppermute(block, axis, [(i - distance, i) for i in devices if i - dist...  48.1 us
    transpose x1, local copies, waits for them, and re-layouts, local(): polar = polarization(g_lesser, jnp.swapaxes(g_greater, 3, 4), NW)[:, :, 0]  8.72 us
  transfers between devices with their start and end apart: 2, of which 1 were waited for; matrix products, arithmetic and copies ran while one was open for 1% of the time, Pallas kernels for 0%

profile of v2, /device:TPU:14, one launch (start us, length us, event | category | flops | bytes accessed | tf_op | source)
XLA Modules:
  0.0 377.5 jit_solution(16571589603924582389)
XLA Ops:
  0.0 0.0 copy-start
  0.0 8.7 %copy.13 = f32[2,16,1,256,256]{4,3,1,0,2:T(8,128)} copy(f32[2,16,1,256,256]{3,4,2,1,0:T(8,128)} %bitcast.54) | data formatting | bytes 16777216 | tf_op jit(solution)/shard_map/transpose | solution.py:238
  8.7 307.1 %shard_map.91 = f32[4,2,4,4,8,8,256]{6,5,4,3,2,1,0:T(8,128)} custom-call(bf16[256,768]{1,0:T(8,128)(2,1)} %constant.18.clone.less_wide, bf16[256,768]{1,0:T(8,128)(2,1)} %constant.19.clone.great_wide, bf16[256,384]{1,0:T(8,128)(2,1)} %constant.20.clone.less_narrow, bf16[256,384]{1,0:T(8,128)(2,1)} %constant.21.clone.great_narrow, ...), custom_call_target="tpu_custom_call" | custom-call | tf_op jit(solution)/shard_map/pallas_call | solution.py:210
  315.8 0.0 copy-start.1
  315.8 4.4 %reduce_sum.9 = f32[2,4,4,8,8,256]{5,4,3,2,1,0:T(8,128)S(1)} reduce(f32[4,2,4,4,8,8,256]{6,5,4,3,2,1,0:T(8,128)} %shard_map.91, f32[]{:T(128)} %constant.8.clone.1), dimensions={0}, to_apply=%region_0.0 | reduce | flops 1572864 | bytes 10485764 | tf_op jit(solution)/shard_map/reduce_sum | solution.py:224
  320.2 0.6 collective-permute-start
  320.8 0.0 copy-done.1
  320.8 0.1 copy.14
  321.0 1.3 collective-permute-start.1
  322.3 0.0 copy-done
  322.3 1.1 fusion.10
  323.3 1.0 fusion.2
  324.4 48.1 %collective-permute-done.1 = f32[1,256,256]{1,2,0:T(8,128)S(1)} collective-permute-done((f32[1,256,256]{1,2,0:T(8,128)S(1)}, f32[1,256,256]{1,2,0:T(8,128)S(1)}, u32[]{:S(2)}, u32[]{:S(2)}) %collective-permute-start.1) | collective-permute-done | bytes 262176 | tf_op jit(solution)/shard_map/ppermute | solution.py:229
  372.5 0.0 collective-permute-done
  372.5 2.6 fusion.7
  375.1 2.4 add_bitcast_fusion
Async XLA Ops:
  0.0 322.3 %copy-start = (f32[1,256,256]{2,1,0:T(8,128)S(1)}, f32[1,256,256]{2,1,0:T(8,128)}, u32[]{:S(2)}) copy-start(f32[1,256,256]{2,1,0:T(8,128)} %param.11) | copy-start | bytes 786436
  315.8 5.0 %copy-start.1 = (f32[1,256,256]{2,1,0:T(8,128)S(1)}, f32[1,256,256]{2,1,0:T(8,128)}, u32[]{:S(2)}) copy-start(f32[1,256,256]{2,1,0:T(8,128)} %param.12) | copy-start | bytes 786436
  320.2 52.2 %collective-permute-start = (f32[2,4,256,256]{3,2,1,0:T(8,128)S(1)}, f32[2,4,256,256]{3,2,1,0:T(8,128)}, u32[]{:S(2)}, u32[]{:S(2)}) collective-permute-start(f32[2,4,256,256]{3,2,1,0:T(8,128)S(1)} %bitcast.55), channel_id=1, source_target_pairs={{0,1},{1,0},{2,3},{3,2},{4,5},{5,4},{6,7},{7,6},{8,9},{9,8},{10,11... | collective-permute-start | bytes 6291464 | tf_op jit(solution)/shard_map/ppermute | solution.py:243
  321.0 51.5 %collective-permute-start.1 = (f32[1,256,256]{1,2,0:T(8,128)S(1)}, f32[1,256,256]{1,2,0:T(8,128)S(1)}, u32[]{:S(2)}, u32[]{:S(2)}) collective-permute-start(f32[1,256,256]{1,2,0:T(8,128)S(1)} %copy.14), channel_id=1, source_target_pairs={{0,1},{2,3},{4,5},{6,7},{8,9},{10,11},{12,13},{14,15},{16,17},{18,... | collective-permute-start | bytes 786440 | tf_op jit(solution)/shard_map/ppermute | solution.py:229
